TPU v7x, 32 devices: a whole 2x2x4 slice. The times are simulated.
32 devices in a mesh: energy: 8 (over z, y), layer: 4 (over x, core).
Axes of the slice: x: 2, y: 2, z: 4, core: 2. Of those that a mesh axis runs over, the one named last changes fastest.
Arguments:
- layer_inverse: float32 [8, 32, 256, 256], P('energy', 'layer'), may hold values from -0.008125 to 1, as said below
- coupling: float32 [256, 256], replicated, may hold values from -0.5125 to 0.5125, as said below
- lead_left: float32 [8, 256, 256], P('energy'), may hold values from -0.0040625 to 0.5, as said below
- lead_right: float32 [8, 256, 256], P('energy'), may hold values from -0.0040625 to 0.5, as said below
- quad_weight: float32 [8], replicated, may hold values from 0.0125 to 0.5
- energy_slot: int32 [8], P('energy'), may hold values from 0 to 7, each once
- plane_of: int32 [32], replicated, may hold values from 0 to 127
- doping: float32 [128, 128, 128], P(('energy', 'layer')), may hold values from -6 to 6
- screening: float32 [128, 128, 128], P(('energy', 'layer')), may hold values from 0.25 to 2
Outputs:
- layer_density: float32 [32, 256], P('layer')
- potential: float32 [128, 128, 128], P(('energy', 'layer'))
- residual: float32 [128, 128, 128], P(('energy', 'layer'))
Inputs may be any that keep to these rules, and one draw needn't show every extreme that they name: `layer_inverse`: each block is symmetric; its diagonal entries lie between 0.3 and 1.0 and its other entries within 0.13 * 256 ** -0.5 of zero. `coupling`: entries are independent with mean zero. `lead_left`: each block is symmetric; its diagonal entries lie between 0.15 and 0.5 and its other entries within 0.065 * 256 ** -0.5 of zero. `lead_right`: each block is symmetric; its diagonal entries lie between 0.15 and 0.5 and its other entries within 0.065 * 256 ** -0.5 of zero. `energy_slot`: every quadrature index appears once. `plane_of`: several layers may share a plane.
All inputs are finite; a program needn't handle non-finite values.
Results may differ from a plain program's by a relative error of at most 0.00018.
Values sent between devices are 32-bit elements; how exact they have to be, the bound alone decides.
A program may use at most 128 MiB of HBM per device.

v0:
```python
import functools
import jax
import jax.numpy as jnp
from jax import lax
from jax.experimental import pallas as pl
from jax.experimental.pallas import tpu as pltpu
from jax.sharding import PartitionSpec as P

ORB_Y = 16
CG_ITERS = 3
CENTER = 7.125
HALF = 7.0
F32 = jnp.float32
BF16 = jnp.bfloat16
MESH = pl.DeviceIdType.MESH


def split(x):
    hi = x.astype(BF16)
    lo = (x - hi.astype(F32)).astype(BF16)
    return hi, lo


def mm(a, b):
    return jnp.dot(a, b, preferred_element_type=F32)


def mm3(a, b):
    return mm(a[0], b[0]) + mm(a[0], b[1]) + mm(a[1], b[0])


def beside_of(v, prev_z, next_z):
    inner = v[1:-1]
    n, ny, nz = inner.shape
    total = v[2:] + v[:-2]
    yi = lax.broadcasted_iota(jnp.int32, (1, ny, 1), 1)
    zi = lax.broadcasted_iota(jnp.int32, (1, 1, nz), 2)
    total += jnp.where(yi == 0, 0.0, pltpu.roll(inner, 1, 1))
    total += jnp.where(yi == ny - 1, 0.0, pltpu.roll(inner, ny - 1, 1))
    total += jnp.where(zi == 0, 0.0, pltpu.roll(inner, 1, 2))
    total += jnp.where(zi == nz - 1, 0.0, pltpu.roll(inner, nz - 1, 2))
    return total


def kernel(
    n_energy, n_layer,
    d_hbm, t_hbm, lead_l_hbm, lead_r_hbm, qw_hbm, slot_ref, plane_hbm, dop_hbm, scr_hbm,
    dens_hbm, vec_hbm, coef_ref,
    dens_ref, vec_ref, out_sem,
    d_ref, t_ref, qw_ref, plane_ref, dop_ref, scr_ref, in_sem,
    prop_ref, ct_ref, c_ref, s_ref, diag_ref, full_ref, gin, gout, dop_ext, scr_ext,
    redbuf, rows_buf, mom,
    relay_send, relay_recv, halo_send, halo_recv,
    red_send, red_recv, row_send, row_recv, mom_send, mom_recv,
):
    steps, m, _ = d_hbm.shape
    planes, ny, nz = dop_hbm.shape
    halo = CG_ITERS
    ext = planes + 2 * halo
    total = n_energy * n_layer
    e = lax.axis_index("energy")
    i = lax.axis_index("layer")
    lin = e * n_layer + i
    up = lax.rem(lin + 1, total)
    down = lax.rem(lin + total - 1, total)
    up_id = (up // n_layer, lax.rem(up, n_layer))
    down_id = (down // n_layer, lax.rem(down, n_layer))

    order = []
    for s in range((steps + 1) // 2):
        order += [s] if s == steps - 1 - s else [s, steps - 1 - s]
    t_copy = pltpu.make_async_copy(t_hbm, t_ref, in_sem.at[steps + 4])
    t_copy.start()
    for s in order:
        pltpu.make_async_copy(d_hbm.at[s], d_ref.at[s], in_sem.at[s]).start()
    grid_copies = [
        pltpu.make_async_copy(qw_hbm, qw_ref, in_sem.at[steps + 5]),
        pltpu.make_async_copy(plane_hbm, plane_ref, in_sem.at[steps + 6]),
        pltpu.make_async_copy(dop_hbm, dop_ref, in_sem.at[steps]),
        pltpu.make_async_copy(scr_hbm, scr_ref, in_sem.at[steps + 1]),
    ]
    for copy in grid_copies:
        copy.start()

    @pl.when(i == 0)
    def _():
        pltpu.make_async_copy(lead_l_hbm, gin.at[0], in_sem.at[steps + 2]).start()

    @pl.when(i == n_layer - 1)
    def _():
        pltpu.make_async_copy(lead_r_hbm, gin.at[1], in_sem.at[steps + 3]).start()

    barrier = pltpu.get_barrier_semaphore()

    def place(k):
        dev = lax.rem(lin + k, total)
        return (dev // n_layer, lax.rem(dev, n_layer))

    def greet(k, c):
        pl.semaphore_signal(barrier, inc=1, device_id=place(k), device_id_type=MESH)
        return c

    lax.fori_loop(1, total, greet, 0)

    halo_copies = []
    for j, (src, dst, width) in enumerate(((dop_ref, dop_ext, halo), (scr_ref, scr_ext, halo - 1))):
        halo_copies.append(pltpu.make_async_remote_copy(
            src_ref=src.at[pl.ds(planes - width, width)], dst_ref=dst.at[pl.ds(halo - width, width)],
            send_sem=halo_send.at[2 * j], recv_sem=halo_recv.at[2 * j],
            device_id=up_id, device_id_type=MESH))
        halo_copies.append(pltpu.make_async_remote_copy(
            src_ref=src.at[pl.ds(0, width)], dst_ref=dst.at[pl.ds(planes + halo, width)],
            send_sem=halo_send.at[2 * j + 1], recv_sem=halo_recv.at[2 * j + 1],
            device_id=down_id, device_id_type=MESH))

    t_copy.wait()
    t = t_ref[...]
    tt = t.T
    t, tt = split(t), split(tt)
    eye = (lax.broadcasted_iota(jnp.int32, (m // 2, m // 2), 0)
           == lax.broadcasted_iota(jnp.int32, (m // 2, m // 2), 1))

    def diag_row(x):
        h = m // 2
        tiles = [jnp.where(eye, x[k * h : k * h + h, k * h : k * h + h], 0.0) for k in range(2)]
        return jnp.concatenate([jnp.sum(tile, axis=0, keepdims=True) for tile in tiles], axis=1)

    sides = ((t, tt), (tt, t))

    def layer_of(side, s):
        return s if side == 0 else steps - 1 - s

    def layer_copy(s):
        return pltpu.make_async_copy(d_hbm.at[s], d_ref.at[s], in_sem.at[s])

    def prepare(s, side):
        d_s = split(d_ref[layer_of(side, s)])
        right, left = sides[side]
        prop = mm3(d_s, right)
        for j, half in enumerate(split(prop)):
            prop_ref[side, j] = half
        for j, half in enumerate(split(prop.T)):
            prop_ref[side, 2 + j] = half

    def advance(s, side, ahead):
        prop = (prop_ref[side, 0], prop_ref[side, 1])
        prop_t = (prop_ref[side, 2], prop_ref[side, 3])
        half = mm3(split(s_ref[side]), prop_t)
        carry = mm3(split(ct_ref[side, s - 1]), prop_t)
        acc = d_ref[layer_of(side, s)] + mm3(prop, split(half))
        ct_ref[side, s] = carry
        s_ref[side] = acc
        diag_ref[side, pl.ds(s, 1), :] = diag_row(acc)
        if side == 0:
            full_ref[pl.ds(s, 1), :] = diag_row(d_ref[s])
        if ahead:
            prepare(s + 1, side)

    def step(s, c):
        for side in range(2):
            advance(s, side, True)
        return c

    def step_wait(s, c):
        layer_copy(s + 1).wait()
        layer_copy(steps - 2 - s).wait()
        return step(s, c)

    for s in (0, 1):
        layer_copy(s).wait()
        layer_copy(steps - 1 - s).wait()
    for side in range(2):
        d = d_ref[layer_of(side, 0)]
        s_ref[side] = d
        ct_ref[side, 0] = mm3(sides[side][1], split(d))
        diag_ref[side, 0:1, :] = diag_row(d)
        if side == 0:
            full_ref[0:1, :] = diag_row(d)
        prepare(1, side)
    lax.fori_loop(1, steps // 2 - 1, step_wait, 0)
    pl.semaphore_wait(barrier, total - 1)
    for copy in grid_copies:
        copy.wait()
    for copy in halo_copies:
        copy.start()
    lax.fori_loop(steps // 2 - 1, steps - 1, step, 0)
    for side in range(2):
        advance(steps - 1, side, False)
        c_ref[side] = ct_ref[side, steps - 1].T

    @pl.when(i == 0)
    def _():
        pltpu.make_async_copy(lead_l_hbm, gin.at[0], in_sem.at[steps + 2]).wait()

    @pl.when(i == n_layer - 1)
    def _():
        pltpu.make_async_copy(lead_r_hbm, gin.at[1], in_sem.at[steps + 3]).wait()

    h = m // 2

    def relay_copy(side, part):
        spot = (pl.ds(0, h), pl.ds(0, m)) if part == 0 else (pl.ds(h, h), pl.ds(h, h))
        return pltpu.make_async_remote_copy(
            src_ref=gout.at[(side,) + spot], dst_ref=gin.at[(side,) + spot],
            send_sem=relay_send.at[side, part], recv_sem=relay_recv.at[side, part],
            device_id=(e, lax.rem(i + 1 - 2 * side + n_layer, n_layer)), device_id_type=MESH)

    first = (2 * i) // n_layer
    def turn_step(turn, c):
        side = first + turn * (1 - 2 * first)
        pos = i + side * (n_layer - 1 - 2 * i)

        @pl.when(pos > 0)
        def _():
            relay_copy(side, 0).wait_recv()
            gin[side, h:, :h] = gin[side, :h, h:].T
            relay_copy(side, 1).wait_recv()

        @pl.when(pos < n_layer - 1)
        def _():
            half = split(mm3(split(gin[side]), split(ct_ref[side, steps - 1])))
            outer = split(c_ref[side])
            gout[side, :h, :] = s_ref[side, :h, :] + mm3([x[:h] for x in outer], half)
            relay_copy(side, 0).start()
            gout[side, h:, h:] = s_ref[side, h:, h:] + mm3([x[h:] for x in outer], [x[:, h:] for x in half])
            relay_copy(side, 1).start()

        g = split(gin[side])
        for s in range(steps):
            carry = ct_ref[side, s]
            z = mm3(g, split(carry))
            diag_ref[side, s : s + 1, :] += jnp.sum(z * carry, axis=0, keepdims=True)
        return c

    lax.fori_loop(0, 2, turn_step, 0)

    n_slots = qw_ref.shape[1]
    pick = lax.broadcasted_iota(jnp.int32, (1, n_slots), 1) == slot_ref[...]
    weight = jnp.sum(jnp.where(pick, qw_ref[...], 0.0), axis=1, keepdims=True)
    back = jnp.concatenate([diag_ref[1, steps - 1 - s : steps - s, :] for s in range(steps)], axis=0)
    redbuf[e] = weight * (diag_ref[0] + back - full_ref[...])

    def red_copy(target, slot, k):
        return pltpu.make_async_remote_copy(
            src_ref=redbuf.at[e], dst_ref=redbuf.at[slot], send_sem=red_send.at[k], recv_sem=red_recv.at[slot],
            device_id=(target, i), device_id_type=MESH)

    def row_copy(target, slot, k):
        return pltpu.make_async_remote_copy(
            src_ref=rows_buf.at[i], dst_ref=rows_buf.at[slot], send_sem=row_send.at[k], recv_sem=row_recv.at[slot],
            device_id=(e, target), device_id_type=MESH)

    def mom_copy(k, slot):
        return pltpu.make_async_remote_copy(
            src_ref=mom.at[lin], dst_ref=mom.at[slot], send_sem=mom_send.at[k], recv_sem=mom_recv.at[slot],
            device_id=place(k), device_id_type=MESH)

    def spread(copy, me, count):
        def send(k, c):
            copy(lax.rem(me + k, count), me, k).start()
            return c

        def receive(k, c):
            peer = lax.rem(me + count - k, count)
            copy(peer, peer, k).wait_recv()
            return c

        lax.fori_loop(1, count, send, 0)
        lax.fori_loop(1, count, receive, 0)

    def finish(copy, me, count):
        def sent(k, c):
            copy(lax.rem(me + k, count), me, k).wait_send()
            return c

        lax.fori_loop(1, count, sent, 0)

    def ordered_sum(ref, count):
        if count <= 8:
            out = ref[0]
            for k in range(1, count):
                out = out + ref[k]
            return out
        return lax.fori_loop(1, count, lambda k, c: c + ref[k], ref[0])

    spread(red_copy, e, n_energy)
    own = ordered_sum(redbuf, n_energy)
    dens_ref[...] = own
    dens_copy = pltpu.make_async_copy(dens_ref, dens_hbm, out_sem.at[0])
    dens_copy.start()
    rows_buf[i] = own
    spread(row_copy, i, n_layer)

    dop_ext[halo : halo + planes] = dop_ref[...]
    scr_ext[halo : halo + planes] = scr_ref[...]
    for copy in halo_copies:
        copy.wait_recv()
    rows = rows_buf[...].reshape(n_layer * steps, m)
    orb_z = m // ORB_Y
    padded = -(-ext // 8) * 8
    first_plane = lin * planes - halo
    ids = first_plane + lax.broadcasted_iota(jnp.int32, (padded, 1), 0)
    onehot = (plane_ref[...] == ids).astype(F32)
    charge_rows = jnp.dot(onehot, rows, precision=lax.Precision.HIGHEST, preferred_element_type=F32)
    ysel = (lax.broadcasted_iota(jnp.int32, (ny, m), 1) // orb_z
            == lax.broadcasted_iota(jnp.int32, (ny, m), 0) // (ny // ORB_Y))
    zsel = (lax.broadcasted_iota(jnp.int32, (m, nz), 1) // (nz // orb_z)
            == lax.rem(lax.broadcasted_iota(jnp.int32, (m, nz), 0), orb_z)).astype(BF16)
    spreads = jnp.concatenate(
        [jnp.where(ysel, charge_rows[p : p + 1, :], 0.0) for p in range(ext)], axis=0)
    hi, lo = split(spreads)
    charge = (mm(hi, zsel) + mm(lo, zsel)).reshape(ext, ny, nz)
    last_plane = total * planes
    gid = first_plane + lax.broadcasted_iota(jnp.int32, (ext, 1, 1), 0)
    inside = jnp.logical_and(gid >= 0, gid < last_plane)
    v0 = jnp.where(inside, charge - dop_ext[...], 0.0)

    basis = [v0]
    for k in range(CG_ITERS):
        prev = basis[-1]
        scr = scr_ext[k + 1 : ext - k - 1]
        shifted = ((6.0 - CENTER + scr) * prev[1:-1] - beside_of(prev, None, None)) * (1.0 / HALF)
        if k > 0:
            shifted = 2.0 * shifted - basis[-2][2:-2]
        mask = inside[k + 1 : ext - k - 1]
        basis.append(jnp.where(mask, shifted, 0.0))
    own_v = [b[halo - k : halo - k + planes] for k, b in enumerate(basis)]
    for k, v in enumerate(own_v):
        vec_ref[k] = v
    vec_copy = pltpu.make_async_copy(vec_ref, vec_hbm, out_sem.at[1])
    vec_copy.start()
    names, parts = {}, []
    for a in range(CG_ITERS):
        for b in range(a, CG_ITERS + 1):
            names[a, b] = len(parts)
            parts.append(jnp.sum(own_v[a] * own_v[b], axis=(0, 1), keepdims=True)[0])
    parts.append(jnp.zeros((16 - len(parts), nz), F32))
    column = jnp.sum(jnp.concatenate(parts, axis=0), axis=1, keepdims=True)
    spot = lax.broadcasted_iota(jnp.int32, (16, nz), 0) == lax.broadcasted_iota(jnp.int32, (16, nz), 1)
    mom[lin] = jnp.sum(jnp.where(spot, column, 0.0), axis=0, keepdims=True)

    def mom_start(k, c):
        mom_copy(k, lin).start()
        return c

    def mom_take(k, c):
        mom_copy(k, lax.rem(lin + total - k, total)).wait_recv()
        return c

    def mom_sent(k, c):
        mom_copy(k, lin).wait_send()
        return c

    lax.fori_loop(1, total, mom_start, 0)
    lax.fori_loop(1, total, mom_take, 0)
    gram = jnp.sum(mom[...].reshape(total, nz), axis=0, keepdims=True)

    def entry(a, b):
        k = names[min(a, b), max(a, b)]
        return gram[:, k : k + 1]

    def inner(x, y):
        terms = [x[a] * y[b] * entry(a, b) for a in x for b in y]
        return functools.reduce(lambda p, q: p + q, terms)

    def add(x, y, scale):
        out = dict(x)
        for k, val in y.items():
            out[k] = out[k] + scale * val if k in out else scale * val
        return out

    def apply(x):
        out = {}
        for k, val in x.items():
            out = add(out, {k: val}, CENTER)
            if k == 0:
                out = add(out, {1: val}, HALF)
            else:
                out = add(out, {k + 1: val, k - 1: val}, 0.5 * HALF)
        return out

    one = jnp.ones((1, 1), F32)
    pot, res, direction = {}, {0: one}, {0: one}
    norm = inner(res, res)
    for it in range(CG_ITERS):
        applied = apply(direction)
        step = norm / inner(direction, applied)
        pot = add(pot, direction, step)
        res = add(res, applied, -step)
        if it + 1 < CG_ITERS:
            new = inner(res, res)
            direction = add(res, direction, new / norm)
            norm = new

    row_ids = lax.broadcasted_iota(jnp.int32, coef_ref.shape, 0)
    lane_ids = lax.broadcasted_iota(jnp.int32, coef_ref.shape, 1)
    table = jnp.zeros(coef_ref.shape, F32)
    for row, coefs in enumerate((pot, res)):
        for k, val in coefs.items():
            table = jnp.where(jnp.logical_and(row_ids == row, lane_ids == k), val, table)
    coef_ref[...] = table

    dens_copy.wait()
    vec_copy.wait()
    for copy in halo_copies:
        copy.wait_send()
    finish(red_copy, e, n_energy)
    finish(row_copy, i, n_layer)
    lax.fori_loop(1, total, mom_sent, 0)
    for side in range(2):
        pos = i + side * (n_layer - 1 - 2 * i)

        @pl.when(pos < n_layer - 1)
        def _():
            relay_copy(side, 0).wait_send()
            relay_copy(side, 1).wait_send()


def combine(own_ref, vec_ref, coef_ref, dens_ref, pot_ref, res_ref):
    dens_ref[...] = own_ref[...]
    for row, out, count in ((0, pot_ref, CG_ITERS), (1, res_ref, CG_ITERS + 1)):
        terms = [coef_ref[row : row + 1, k : k + 1][None] * vec_ref[k] for k in range(count)]
        out[...] = functools.reduce(lambda p, q: p + q, terms)


def body(n_energy, n_layer, layer_inverse, coupling, lead_left, lead_right, quad_weight,
         energy_slot, plane_of, doping, screening):
    steps, m = layer_inverse.shape[1], layer_inverse.shape[2]
    planes, ny, nz = doping.shape
    ext = planes + 2 * CG_ITERS
    dma = pltpu.SemaphoreType.DMA
    vmem = pl.BlockSpec(memory_space=pltpu.VMEM)
    anym = pl.BlockSpec(memory_space=pltpu.HBM)
    call = pl.pallas_call(
        functools.partial(kernel, n_energy, n_layer),
        out_shape=(
            jax.ShapeDtypeStruct((steps, m), F32),
            jax.ShapeDtypeStruct((CG_ITERS + 1,) + doping.shape, F32),
            jax.ShapeDtypeStruct((8, 128), F32),
        ),
        in_specs=[anym] * 5 + [vmem] + [anym] * 3,
        out_specs=(anym, anym, vmem),
        scratch_shapes=[
            pltpu.VMEM((steps, m), F32),
            pltpu.VMEM((CG_ITERS + 1,) + doping.shape, F32),
            dma((2,)),
            pltpu.VMEM((steps, m, m), F32),
            pltpu.VMEM((m, m), F32),
            pltpu.VMEM((1,) + quad_weight.shape, F32),
            pltpu.VMEM((1,) + plane_of.shape, jnp.int32),
            pltpu.VMEM(doping.shape, F32),
            pltpu.VMEM(doping.shape, F32),
            dma((steps + 7,)),
            pltpu.VMEM((2, 4, m, m), BF16),
            pltpu.VMEM((2, steps, m, m), F32),
            pltpu.VMEM((2, m, m), F32),
            pltpu.VMEM((2, m, m), F32),
            pltpu.VMEM((2, steps, m), F32),
            pltpu.VMEM((steps, m), F32),
            pltpu.VMEM((2, m, m), F32),
            pltpu.VMEM((2, m, m), F32),
            pltpu.VMEM((ext, ny, nz), F32),
            pltpu.VMEM((ext, ny, nz), F32),
            pltpu.VMEM((n_energy, steps, m), F32),
            pltpu.VMEM((n_layer, steps, m), F32),
            pltpu.VMEM((n_energy * n_layer, 1, nz), F32),
            dma((2, 2)), dma((2, 2)), dma((4,)), dma((4,)),
            dma((n_energy,)), dma((n_energy,)), dma((n_layer,)), dma((n_layer,)),
            dma((n_energy * n_layer,)), dma((n_energy * n_layer,)),
        ],
        compiler_params=pltpu.CompilerParams(
            collective_id=0, has_side_effects=True, vmem_limit_bytes=67_000_000
        ),
    )
    own, vecs, coefs = call(
        layer_inverse[0], coupling, lead_left[0], lead_right[0], quad_weight[None, :],
        energy_slot[:, None], plane_of[None, :], doping, screening,
    )
    return pl.pallas_call(
        combine,
        out_shape=(
            jax.ShapeDtypeStruct((steps, m), F32),
            jax.ShapeDtypeStruct(doping.shape, F32),
            jax.ShapeDtypeStruct(doping.shape, F32),
        ),
        in_specs=[vmem] * 3,
        out_specs=(vmem, vmem, vmem),
        compiler_params=pltpu.CompilerParams(vmem_limit_bytes=67_000_000),
    )(own, vecs, coefs)


def solution(mesh):
    in_specs = (
        P("energy", "layer", None, None),
        P(),
        P("energy", None, None),
        P("energy", None, None),
        P(),
        P("energy"),
        P(),
        P(("energy", "layer"), None, None),
        P(("energy", "layer"), None, None),
    )
    out_specs = (
        P("layer", None),
        P(("energy", "layer"), None, None),
        P(("energy", "layer"), None, None),
    )
    run = functools.partial(body, mesh.shape["energy"], mesh.shape["layer"])
    return jax.shard_map(run, mesh=mesh, in_specs=in_specs, out_specs=out_specs, check_vma=False)
```

profile of v0, /device:TPU:0, one launch (start us, length us, event | category | flops | bytes accessed | tf_op | source)
XLA Modules:
  0.0 41.0 jit_solution(2661525683350217404)
XLA Ops:
  1.3 37.5 %shard_map.112 = (f32[8,256]{1,0:T(8,128)}, f32[4,4,128,128]{3,2,1,0:T(8,128)}, f32[8,128]{1,0:T(8,128)}) custom-call(f32[8,256,256]{2,1,0:T(8,128)} %bitcast.7, f32[256,256]{1,0:T(8,128)} %t_hbm.1, f32[256,256]{1,0:T(8,128)} %bitcast.8, f32[256,256]{1,0:T(8,128)} %bitcast.9, f32[1,8]{1,0:T(1,128)} %bitcast.10, s32[1,1]{1,0:T(1,128)} %bitcast.6.slot_ref, ...), custom_call_target="tpu_custom_call" | custom-call | tf_op jit(solution)/shard_map/pallas_call | solution.py:475
  38.8 2.2 %shard_map.113 = (f32[8,256]{1,0:T(8,128)}, f32[4,128,128]{2,1,0:T(8,128)}, f32[4,128,128]{2,1,0:T(8,128)}) custom-call(f32[8,256]{1,0:T(8,128)} %get-tuple-element.6.own_ref, f32[4,4,128,128]{3,2,1,0:T(8,128)} %get-tuple-element.7.vec_ref, f32[8,128]{1,0:T(8,128)} %get-tuple-element.8.coef_ref), custom_call_target="tpu_custom_call" | custom-call | tf_op jit(solution)/shard_map/pallas_call | solution.py:479
where the time goes:
time: 41.2 us; the launch traced here: 41 us
  Pallas kernels  39.8 us (97%)
  between operations  1.29 us (3%)
    pallas_call x1, Pallas kernels, body(): call(layer_inverse[0], coupling, lead_left[0], lead_right[0], quad_weight...  37.5 us
    pallas_call x1, Pallas kernels, body(): pl.pallas_call(combine, out_shape=(jax.ShapeDtypeStruct((steps, m), F32),...  2.22 us

commit v1 on v0

--- a/solution.py
+++ b/solution.py
@@ -12,7 +12,7 @@
 HALF = 7.0
 F32 = jnp.float32
 BF16 = jnp.bfloat16
-MESH = pl.DeviceIdType.MESH
+LOGICAL = pl.DeviceIdType.LOGICAL
 
 
 def split(x):
@@ -27,6 +27,14 @@
 
 def mm3(a, b):
     return mm(a[0], b[0]) + mm(a[0], b[1]) + mm(a[1], b[0])
+
+
+def loop(count, step):
+    if count <= 32:
+        for k in range(1, count):
+            step(k, 0)
+    else:
+        lax.fori_loop(1, count, step, 0)
 
 
 def beside_of(v, prev_z, next_z):
@@ -45,8 +53,7 @@
 def kernel(
     n_energy, n_layer,
     d_hbm, t_hbm, lead_l_hbm, lead_r_hbm, qw_hbm, slot_ref, plane_hbm, dop_hbm, scr_hbm,
-    dens_hbm, vec_hbm, coef_ref,
-    dens_ref, vec_ref, out_sem,
+    dens_ref, pot_ref, res_ref,
     d_ref, t_ref, qw_ref, plane_ref, dop_ref, scr_ref, in_sem,
     prop_ref, ct_ref, c_ref, s_ref, diag_ref, full_ref, gin, gout, dop_ext, scr_ext,
     redbuf, rows_buf, mom,
@@ -63,8 +70,6 @@
     lin = e * n_layer + i
     up = lax.rem(lin + 1, total)
     down = lax.rem(lin + total - 1, total)
-    up_id = (up // n_layer, lax.rem(up, n_layer))
-    down_id = (down // n_layer, lax.rem(down, n_layer))
 
     order = []
     for s in range((steps + 1) // 2):
@@ -92,26 +97,22 @@
 
     barrier = pltpu.get_barrier_semaphore()
 
-    def place(k):
-        dev = lax.rem(lin + k, total)
-        return (dev // n_layer, lax.rem(dev, n_layer))
-
     def greet(k, c):
-        pl.semaphore_signal(barrier, inc=1, device_id=place(k), device_id_type=MESH)
+        pl.semaphore_signal(barrier, inc=1, device_id=lax.rem(lin + k, total), device_id_type=LOGICAL)
         return c
 
-    lax.fori_loop(1, total, greet, 0)
+    loop(total, greet)
 
     halo_copies = []
     for j, (src, dst, width) in enumerate(((dop_ref, dop_ext, halo), (scr_ref, scr_ext, halo - 1))):
         halo_copies.append(pltpu.make_async_remote_copy(
             src_ref=src.at[pl.ds(planes - width, width)], dst_ref=dst.at[pl.ds(halo - width, width)],
             send_sem=halo_send.at[2 * j], recv_sem=halo_recv.at[2 * j],
-            device_id=up_id, device_id_type=MESH))
+            device_id=up, device_id_type=LOGICAL))
         halo_copies.append(pltpu.make_async_remote_copy(
             src_ref=src.at[pl.ds(0, width)], dst_ref=dst.at[pl.ds(planes + halo, width)],
             send_sem=halo_send.at[2 * j + 1], recv_sem=halo_recv.at[2 * j + 1],
-            device_id=down_id, device_id_type=MESH))
+            device_id=down, device_id_type=LOGICAL))
 
     t_copy.wait()
     t = t_ref[...]
@@ -203,7 +204,7 @@
         return pltpu.make_async_remote_copy(
             src_ref=gout.at[(side,) + spot], dst_ref=gin.at[(side,) + spot],
             send_sem=relay_send.at[side, part], recv_sem=relay_recv.at[side, part],
-            device_id=(e, lax.rem(i + 1 - 2 * side + n_layer, n_layer)), device_id_type=MESH)
+            device_id=e * n_layer + lax.rem(i + 1 - 2 * side + n_layer, n_layer), device_id_type=LOGICAL)
 
     first = (2 * i) // n_layer
     def turn_step(turn, c):
@@ -240,40 +241,18 @@
     back = jnp.concatenate([diag_ref[1, steps - 1 - s : steps - s, :] for s in range(steps)], axis=0)
     redbuf[e] = weight * (diag_ref[0] + back - full_ref[...])
 
-    def red_copy(target, slot, k):
+    def exchange(buf, me, count, place, send_sem, recv_sem):
+        def send(k, c):
+            pltpu.make_async_remote_copy(
+                src_ref=buf.at[me], dst_ref=buf.at[me], send_sem=send_sem, recv_sem=recv_sem,
+                device_id=place(lax.rem(me + k, count)), device_id_type=LOGICAL).start()
+            return c
+
+        loop(count, send)
+        rest = buf.at[pl.ds(0, count - 1)]
         return pltpu.make_async_remote_copy(
-            src_ref=redbuf.at[e], dst_ref=redbuf.at[slot], send_sem=red_send.at[k], recv_sem=red_recv.at[slot],
-            device_id=(target, i), device_id_type=MESH)
-
-    def row_copy(target, slot, k):
-        return pltpu.make_async_remote_copy(
-            src_ref=rows_buf.at[i], dst_ref=rows_buf.at[slot], send_sem=row_send.at[k], recv_sem=row_recv.at[slot],
-            device_id=(e, target), device_id_type=MESH)
-
-    def mom_copy(k, slot):
-        return pltpu.make_async_remote_copy(
-            src_ref=mom.at[lin], dst_ref=mom.at[slot], send_sem=mom_send.at[k], recv_sem=mom_recv.at[slot],
-            device_id=place(k), device_id_type=MESH)
-
-    def spread(copy, me, count):
-        def send(k, c):
-            copy(lax.rem(me + k, count), me, k).start()
-            return c
-
-        def receive(k, c):
-            peer = lax.rem(me + count - k, count)
-            copy(peer, peer, k).wait_recv()
-            return c
-
-        lax.fori_loop(1, count, send, 0)
-        lax.fori_loop(1, count, receive, 0)
-
-    def finish(copy, me, count):
-        def sent(k, c):
-            copy(lax.rem(me + k, count), me, k).wait_send()
-            return c
-
-        lax.fori_loop(1, count, sent, 0)
+            src_ref=rest, dst_ref=rest, send_sem=send_sem, recv_sem=recv_sem,
+            device_id=place(lax.rem(me + 1, count)), device_id_type=LOGICAL)
 
     def ordered_sum(ref, count):
         if count <= 8:
@@ -283,13 +262,15 @@
             return out
         return lax.fori_loop(1, count, lambda k, c: c + ref[k], ref[0])
 
-    spread(red_copy, e, n_energy)
+    red = exchange(redbuf, e, n_energy, lambda p: p * n_layer + i, red_send, red_recv)
+    red.wait_recv()
     own = ordered_sum(redbuf, n_energy)
     dens_ref[...] = own
-    dens_copy = pltpu.make_async_copy(dens_ref, dens_hbm, out_sem.at[0])
-    dens_copy.start()
     rows_buf[i] = own
-    spread(row_copy, i, n_layer)
+    row = exchange(rows_buf, i, n_layer, lambda p: e * n_layer + p, row_send, row_recv)
+    red.wait_send()
+    row.wait_recv()
+    row.wait_send()
 
     dop_ext[halo : halo + planes] = dop_ref[...]
     scr_ext[halo : halo + planes] = scr_ref[...]
@@ -325,10 +306,6 @@
         mask = inside[k + 1 : ext - k - 1]
         basis.append(jnp.where(mask, shifted, 0.0))
     own_v = [b[halo - k : halo - k + planes] for k, b in enumerate(basis)]
-    for k, v in enumerate(own_v):
-        vec_ref[k] = v
-    vec_copy = pltpu.make_async_copy(vec_ref, vec_hbm, out_sem.at[1])
-    vec_copy.start()
     names, parts = {}, []
     for a in range(CG_ITERS):
         for b in range(a, CG_ITERS + 1):
@@ -339,20 +316,19 @@
     spot = lax.broadcasted_iota(jnp.int32, (16, nz), 0) == lax.broadcasted_iota(jnp.int32, (16, nz), 1)
     mom[lin] = jnp.sum(jnp.where(spot, column, 0.0), axis=0, keepdims=True)
 
-    def mom_start(k, c):
-        mom_copy(k, lin).start()
-        return c
-
-    def mom_take(k, c):
-        mom_copy(k, lax.rem(lin + total - k, total)).wait_recv()
-        return c
-
-    def mom_sent(k, c):
-        mom_copy(k, lin).wait_send()
-        return c
-
-    lax.fori_loop(1, total, mom_start, 0)
-    lax.fori_loop(1, total, mom_take, 0)
+    sums = exchange(mom, lin, total, lambda p: p, mom_send, mom_recv)
+    for copy in halo_copies:
+        copy.wait_send()
+    sums.wait_send()
+    for side in range(2):
+        pos = i + side * (n_layer - 1 - 2 * i)
+
+        @pl.when(pos < n_layer - 1)
+        def _():
+            relay_copy(side, 0).wait_send()
+            relay_copy(side, 1).wait_send()
+
+    sums.wait_recv()
     gram = jnp.sum(mom[...].reshape(total, nz), axis=0, keepdims=True)
 
     def entry(a, b):
@@ -392,35 +368,20 @@
             direction = add(res, direction, new / norm)
             norm = new
 
-    row_ids = lax.broadcasted_iota(jnp.int32, coef_ref.shape, 0)
-    lane_ids = lax.broadcasted_iota(jnp.int32, coef_ref.shape, 1)
-    table = jnp.zeros(coef_ref.shape, F32)
-    for row, coefs in enumerate((pot, res)):
-        for k, val in coefs.items():
-            table = jnp.where(jnp.logical_and(row_ids == row, lane_ids == k), val, table)
-    coef_ref[...] = table
-
-    dens_copy.wait()
-    vec_copy.wait()
-    for copy in halo_copies:
-        copy.wait_send()
-    finish(red_copy, e, n_energy)
-    finish(row_copy, i, n_layer)
-    lax.fori_loop(1, total, mom_sent, 0)
-    for side in range(2):
-        pos = i + side * (n_layer - 1 - 2 * i)
-
-        @pl.when(pos < n_layer - 1)
-        def _():
-            relay_copy(side, 0).wait_send()
-            relay_copy(side, 1).wait_send()
-
-
-def combine(own_ref, vec_ref, coef_ref, dens_ref, pot_ref, res_ref):
-    dens_ref[...] = own_ref[...]
-    for row, out, count in ((0, pot_ref, CG_ITERS), (1, res_ref, CG_ITERS + 1)):
-        terms = [coef_ref[row : row + 1, k : k + 1][None] * vec_ref[k] for k in range(count)]
+    for coefs, out in ((pot, pot_ref), (res, res_ref)):
+        terms = [coefs[k][None] * own_v[k] for k in coefs]
         out[...] = functools.reduce(lambda p, q: p + q, terms)
+
+
+def put(dens_ref, pot_ref, res_ref, dens_hbm, pot_hbm, res_hbm, sem):
+    copies = [
+        pltpu.make_async_copy(src, dst, sem.at[k])
+        for k, (src, dst) in enumerate(((pot_ref, pot_hbm), (res_ref, res_hbm), (dens_ref, dens_hbm)))
+    ]
+    for copy in copies:
+        copy.start()
+    for copy in copies:
+        copy.wait()
 
 
 def body(n_energy, n_layer, layer_inverse, coupling, lead_left, lead_right, quad_weight,
@@ -433,17 +394,10 @@
     anym = pl.BlockSpec(memory_space=pltpu.HBM)
     call = pl.pallas_call(
         functools.partial(kernel, n_energy, n_layer),
-        out_shape=(
-            jax.ShapeDtypeStruct((steps, m), F32),
-            jax.ShapeDtypeStruct((CG_ITERS + 1,) + doping.shape, F32),
-            jax.ShapeDtypeStruct((8, 128), F32),
-        ),
+        out_shape=(pltpu.VMEM((steps, m), F32), pltpu.VMEM(doping.shape, F32), pltpu.VMEM(doping.shape, F32)),
         in_specs=[anym] * 5 + [vmem] + [anym] * 3,
-        out_specs=(anym, anym, vmem),
+        out_specs=(vmem, vmem, vmem),
         scratch_shapes=[
-            pltpu.VMEM((steps, m), F32),
-            pltpu.VMEM((CG_ITERS + 1,) + doping.shape, F32),
-            dma((2,)),
             pltpu.VMEM((steps, m, m), F32),
             pltpu.VMEM((m, m), F32),
             pltpu.VMEM((1,) + quad_weight.shape, F32),
@@ -465,28 +419,24 @@
             pltpu.VMEM((n_layer, steps, m), F32),
             pltpu.VMEM((n_energy * n_layer, 1, nz), F32),
             dma((2, 2)), dma((2, 2)), dma((4,)), dma((4,)),
-            dma((n_energy,)), dma((n_energy,)), dma((n_layer,)), dma((n_layer,)),
-            dma((n_energy * n_layer,)), dma((n_energy * n_layer,)),
+            dma, dma, dma, dma, dma, dma,
         ],
         compiler_params=pltpu.CompilerParams(
-            collective_id=0, has_side_effects=True, vmem_limit_bytes=67_000_000
+            collective_id=0, has_side_effects=True, vmem_limit_bytes=66_000_000
         ),
     )
-    own, vecs, coefs = call(
+    inner = call(
         layer_inverse[0], coupling, lead_left[0], lead_right[0], quad_weight[None, :],
         energy_slot[:, None], plane_of[None, :], doping, screening,
     )
     return pl.pallas_call(
-        combine,
-        out_shape=(
-            jax.ShapeDtypeStruct((steps, m), F32),
-            jax.ShapeDtypeStruct(doping.shape, F32),
-            jax.ShapeDtypeStruct(doping.shape, F32),
-        ),
+        put,
+        out_shape=tuple(jax.ShapeDtypeStruct(x.shape, F32) for x in inner),
         in_specs=[vmem] * 3,
-        out_specs=(vmem, vmem, vmem),
-        compiler_params=pltpu.CompilerParams(vmem_limit_bytes=67_000_000),
-    )(own, vecs, coefs)
+        out_specs=(anym, anym, anym),
+        scratch_shapes=[dma((3,))],
+        compiler_params=pltpu.CompilerParams(vmem_limit_bytes=1_000_000),
+    )(*(pltpu.with_memory_space_constraint(x, pltpu.VMEM) for x in inner))
 
 
 def solution(mesh):

time: 41.2 us -> 37.8 us (0.917)
  Pallas kernels: 39.8 us -> 36.3 us
    pallas_call x1, Pallas kernels: 37.5 us -> 35.5 us  [body(): call(layer_inverse[0], coupling, lead_left[0], lead_right[0], quad_weight...]
    pallas_call x1, Pallas kernels: 2.22 us -> 0.82 us  [body(): pl.pallas_call(put, out_shape=tuple((jax.ShapeDtypeStruct(x.shape, F32) f...]
where the time goes in v1:
time: 37.8 us; the launch traced here: 37.6 us
  Pallas kernels  36.3 us (96%)
  between operations  1.29 us (3%)
    pallas_call x1, Pallas kernels, body(): call(layer_inverse[0], coupling, lead_left[0], lead_right[0], quad_weight...  35.5 us
    pallas_call x1, Pallas kernels, body(): pl.pallas_call(put, out_shape=tuple((jax.ShapeDtypeStruct(x.shape, F32) f...  0.82 us

profile of v1, /device:TPU:0, one launch (start us, length us, event | category | flops | bytes accessed | tf_op | source)
XLA Modules:
  0.0 37.6 jit_solution(11591335550075406358)
XLA Ops:
  1.3 35.5 %shard_map.112 = (f32[8,256]{1,0:T(8,128)S(1)}, f32[4,128,128]{2,1,0:T(8,128)S(1)}, f32[4,128,128]{2,1,0:T(8,128)S(1)}) custom-call(f32[8,256,256]{2,1,0:T(8,128)} %bitcast.7, f32[256,256]{1,0:T(8,128)} %t_hbm.1, f32[256,256]{1,0:T(8,128)} %bitcast.8, f32[256,256]{1,0:T(8,128)} %bitcast.9, f32[1,8]{1,0:T(1,128)} %bitcast.10, s32[1,1]{1,0:T(1,128)} %bitcast.6.slot_ref, ...), custom_call_target="tpu_custom_call" | custom-call | tf_op jit(solution)/shard_map/pallas_call | solution.py:428
  36.8 0.8 %shard_map.113 = (f32[8,256]{1,0:T(8,128)}, f32[4,128,128]{2,1,0:T(8,128)}, f32[4,128,128]{2,1,0:T(8,128)}) custom-call(f32[8,256]{1,0:T(8,128)S(1)} %get-tuple-element.6.dens_ref, f32[4,128,128]{2,1,0:T(8,128)S(1)} %get-tuple-element.7.pot_ref, f32[4,128,128]{2,1,0:T(8,128)S(1)} %get-tuple-element.8.res_ref), custom_call_target="tpu_custom_call" | custom-call | tf_op jit(solution)/shard_map/pallas_call | solution.py:432

commit v2 on v1

--- a/solution.py
+++ b/solution.py
@@ -25,8 +25,12 @@
     return jnp.dot(a, b, preferred_element_type=F32)
 
 
-def mm3(a, b):
-    return mm(a[0], b[0]) + mm(a[0], b[1]) + mm(a[1], b[0])
+def mm3(a, b, dot=mm):
+    return dot(a[0], b[0]) + dot(a[0], b[1]) + dot(a[1], b[0])
+
+
+def mmt(a, b):
+    return lax.dot_general(a, b, (((1,), (1,)), ((), ())), preferred_element_type=F32)
 
 
 def loop(count, step):
@@ -52,13 +56,13 @@
 
 def kernel(
     n_energy, n_layer,
-    d_hbm, t_hbm, lead_l_hbm, lead_r_hbm, qw_hbm, slot_ref, plane_hbm, dop_hbm, scr_hbm,
+    d_hbm, t_hbm, lead_l_hbm, lead_r_hbm, qw_hbm, slot_hbm, plane_hbm, dop_hbm, scr_hbm,
     dens_ref, pot_ref, res_ref,
-    d_ref, t_ref, qw_ref, plane_ref, dop_ref, scr_ref, in_sem,
-    prop_ref, ct_ref, c_ref, s_ref, diag_ref, full_ref, gin, gout, dop_ext, scr_ext,
-    redbuf, rows_buf, mom,
+    d_ref, t_ref, qw_ref, slot_ref, plane_ref, dop_ref, scr_ref, in_sem,
+    p_ref, s_ref, ct_ref, c_ref, w_ref, x_ref, diag_ref, full_ref, gin, gout, dop_ext, scr_ext,
+    zbuf, redbuf, mom,
     relay_send, relay_recv, halo_send, halo_recv,
-    red_send, red_recv, row_send, row_recv, mom_send, mom_recv,
+    z_send, z_recv, red_send, red_recv, mom_send, mom_recv,
 ):
     steps, m, _ = d_hbm.shape
     planes, ny, nz = dop_hbm.shape
@@ -76,24 +80,29 @@
         order += [s] if s == steps - 1 - s else [s, steps - 1 - s]
     t_copy = pltpu.make_async_copy(t_hbm, t_ref, in_sem.at[steps + 4])
     t_copy.start()
-    for s in order:
-        pltpu.make_async_copy(d_hbm.at[s], d_ref.at[s], in_sem.at[s]).start()
+
+    def layer_copy(s):
+        return pltpu.make_async_copy(d_hbm.at[s], d_ref.at[s], in_sem.at[s])
+
+    def lead_copy(side):
+        return pltpu.make_async_copy((lead_l_hbm, lead_r_hbm)[side], s_ref.at[side], in_sem.at[steps + 2 + side])
+
+    ends = (0, n_layer - 1)
+    for s in order[:2]:
+        layer_copy(s).start()
+    for side in range(2):
+        pl.when(i == ends[side])(lead_copy(side).start)
+    for s in order[2:]:
+        layer_copy(s).start()
     grid_copies = [
         pltpu.make_async_copy(qw_hbm, qw_ref, in_sem.at[steps + 5]),
         pltpu.make_async_copy(plane_hbm, plane_ref, in_sem.at[steps + 6]),
+        pltpu.make_async_copy(slot_hbm, slot_ref, in_sem.at[steps + 7]),
         pltpu.make_async_copy(dop_hbm, dop_ref, in_sem.at[steps]),
         pltpu.make_async_copy(scr_hbm, scr_ref, in_sem.at[steps + 1]),
     ]
     for copy in grid_copies:
         copy.start()
-
-    @pl.when(i == 0)
-    def _():
-        pltpu.make_async_copy(lead_l_hbm, gin.at[0], in_sem.at[steps + 2]).start()
-
-    @pl.when(i == n_layer - 1)
-    def _():
-        pltpu.make_async_copy(lead_r_hbm, gin.at[1], in_sem.at[steps + 3]).start()
 
     barrier = pltpu.get_barrier_semaphore()
 
@@ -127,110 +136,113 @@
         return jnp.concatenate([jnp.sum(tile, axis=0, keepdims=True) for tile in tiles], axis=1)
 
     sides = ((t, tt), (tt, t))
+    h = m // 2
+    last = steps - 1
 
     def layer_of(side, s):
-        return s if side == 0 else steps - 1 - s
-
-    def layer_copy(s):
-        return pltpu.make_async_copy(d_hbm.at[s], d_ref.at[s], in_sem.at[s])
+        return s if side == 0 else last - s
+
+    def pair(ref, at):
+        return ref[at + (0,)], ref[at + (1,)]
 
     def prepare(s, side):
-        d_s = split(d_ref[layer_of(side, s)])
-        right, left = sides[side]
-        prop = mm3(d_s, right)
-        for j, half in enumerate(split(prop)):
-            prop_ref[side, j] = half
-        for j, half in enumerate(split(prop.T)):
-            prop_ref[side, 2 + j] = half
-
-    def advance(s, side, ahead):
-        prop = (prop_ref[side, 0], prop_ref[side, 1])
-        prop_t = (prop_ref[side, 2], prop_ref[side, 3])
-        half = mm3(split(s_ref[side]), prop_t)
-        carry = mm3(split(ct_ref[side, s - 1]), prop_t)
-        acc = d_ref[layer_of(side, s)] + mm3(prop, split(half))
-        ct_ref[side, s] = carry
-        s_ref[side] = acc
-        diag_ref[side, pl.ds(s, 1), :] = diag_row(acc)
-        if side == 0:
-            full_ref[pl.ds(s, 1), :] = diag_row(d_ref[s])
-        if ahead:
-            prepare(s + 1, side)
-
-    def step(s, c):
+        prop = mm3(split(d_ref[layer_of(side, s)]), sides[side][0])
+        for j, x in enumerate(split(prop)):
+            p_ref[side, s % 2, j] = x
+
+    def store_carry(s, side, ct):
+        hi, lo = split(ct)
+        ct_ref[side, s, 0] = hi
+        ct_ref[side, s, 1] = lo
+        w_ref[side, s] = 2.0 * ct - hi.astype(F32)
+
+    for side in range(2):
+        @pl.when(i != ends[side])
+        def _():
+            s_ref[side] = jnp.zeros((m, m), F32)
+    for s in order[:2]:
+        layer_copy(s).wait()
+    for side in range(2):
+        prepare(0, side)
+    for s in order[2:]:
+        layer_copy(s).wait()
+    for side in range(2):
+        pl.when(i == ends[side])(lead_copy(side).wait)
+
+    for s in range(steps):
+        props = [pair(p_ref, (side, s % 2)) for side in range(2)]
+        halves = [mm3(props[side], split(s_ref[side])) for side in range(2)]
+        if s < last:
+            for side in range(2):
+                prepare(s + 1, side)
         for side in range(2):
-            advance(s, side, True)
-        return c
-
-    def step_wait(s, c):
-        layer_copy(s + 1).wait()
-        layer_copy(steps - 2 - s).wait()
-        return step(s, c)
-
-    for s in (0, 1):
-        layer_copy(s).wait()
-        layer_copy(steps - 1 - s).wait()
-    for side in range(2):
-        d = d_ref[layer_of(side, 0)]
-        s_ref[side] = d
-        ct_ref[side, 0] = mm3(sides[side][1], split(d))
-        diag_ref[side, 0:1, :] = diag_row(d)
-        if side == 0:
-            full_ref[0:1, :] = diag_row(d)
-        prepare(1, side)
-    lax.fori_loop(1, steps // 2 - 1, step_wait, 0)
-    pl.semaphore_wait(barrier, total - 1)
-    for copy in grid_copies:
-        copy.wait()
-    for copy in halo_copies:
-        copy.start()
-    lax.fori_loop(steps // 2 - 1, steps - 1, step, 0)
-    for side in range(2):
-        advance(steps - 1, side, False)
-        c_ref[side] = ct_ref[side, steps - 1].T
-
-    @pl.when(i == 0)
-    def _():
-        pltpu.make_async_copy(lead_l_hbm, gin.at[0], in_sem.at[steps + 2]).wait()
-
-    @pl.when(i == n_layer - 1)
-    def _():
-        pltpu.make_async_copy(lead_r_hbm, gin.at[1], in_sem.at[steps + 3]).wait()
-
-    h = m // 2
-
-    def relay_copy(side, part):
+            d = d_ref[layer_of(side, s)]
+            acc = d + mm3(split(halves[side]), props[side], mmt)
+            s_ref[side] = acc
+            diag_ref[side, s : s + 1, :] = diag_row(acc)
+            if side == 0:
+                full_ref[s : s + 1, :] = diag_row(d)
+        for side in range(2):
+            if s == 0:
+                hi, lo = (x.T for x in props[side])
+                ct_ref[side, 0, 0] = hi
+                ct_ref[side, 0, 1] = lo
+                w_ref[side, 0] = hi.astype(F32) + 2.0 * lo.astype(F32)
+            else:
+                store_carry(s, side, mm3(pair(ct_ref, (side, s - 1)), props[side], mmt))
+        if s == 1:
+            pl.semaphore_wait(barrier, total - 1)
+            for copy in grid_copies:
+                copy.wait()
+            for copy in halo_copies:
+                copy.start()
+
+    def relay_copy(side, part, buf):
         spot = (pl.ds(0, h), pl.ds(0, m)) if part == 0 else (pl.ds(h, h), pl.ds(h, h))
         return pltpu.make_async_remote_copy(
-            src_ref=gout.at[(side,) + spot], dst_ref=gin.at[(side,) + spot],
+            src_ref=buf.at[spot], dst_ref=gin.at[(side,) + spot],
             send_sem=relay_send.at[side, part], recv_sem=relay_recv.at[side, part],
             device_id=e * n_layer + lax.rem(i + 1 - 2 * side + n_layer, n_layer), device_id_type=LOGICAL)
 
+    for side in range(2):
+        @pl.when(i == ends[side])
+        def _():
+            for part in range(2):
+                relay_copy(side, part, s_ref.at[side]).start()
+
+    for side in range(2):
+        for part in range(2):
+            c_ref[side, part] = ct_ref[side, last, part].T
+
     first = (2 * i) // n_layer
+
     def turn_step(turn, c):
         side = first + turn * (1 - 2 * first)
         pos = i + side * (n_layer - 1 - 2 * i)
 
         @pl.when(pos > 0)
         def _():
-            relay_copy(side, 0).wait_recv()
+            relay_copy(side, 0, gout.at[side]).wait_recv()
             gin[side, h:, :h] = gin[side, :h, h:].T
-            relay_copy(side, 1).wait_recv()
-
-        @pl.when(pos < n_layer - 1)
-        def _():
-            half = split(mm3(split(gin[side]), split(ct_ref[side, steps - 1])))
-            outer = split(c_ref[side])
-            gout[side, :h, :] = s_ref[side, :h, :] + mm3([x[:h] for x in outer], half)
-            relay_copy(side, 0).start()
-            gout[side, h:, h:] = s_ref[side, h:, h:] + mm3([x[h:] for x in outer], [x[:, h:] for x in half])
-            relay_copy(side, 1).start()
-
-        g = split(gin[side])
-        for s in range(steps):
-            carry = ct_ref[side, s]
-            z = mm3(g, split(carry))
-            diag_ref[side, s : s + 1, :] += jnp.sum(z * carry, axis=0, keepdims=True)
+            relay_copy(side, 1, gout.at[side]).wait_recv()
+            for part, x in enumerate(split(gin[side])):
+                x_ref[part] = x
+
+            @pl.when(pos < n_layer - 1)
+            def _():
+                half = split(mm3((x_ref[0], x_ref[1]), pair(ct_ref, (side, last))))
+                outer = pair(c_ref, (side,))
+                gout[side, :h, :] = s_ref[side, :h, :] + mm3([x[:h] for x in outer], half)
+                relay_copy(side, 0, gout.at[side]).start()
+                gout[side, h:, h:] = (
+                    s_ref[side, h:, h:] + mm3([x[h:] for x in outer], [x[:, h:] for x in half]))
+                relay_copy(side, 1, gout.at[side]).start()
+
+            for s in range(steps):
+                carry = ct_ref[side, s, 0]
+                z = mm(x_ref[0], carry) + mm(x_ref[1], carry)
+                diag_ref[side, s : s + 1, :] += jnp.sum(z * w_ref[side, s], axis=0, keepdims=True)
+
         return c
 
     lax.fori_loop(0, 2, turn_step, 0)
@@ -239,7 +251,12 @@
     pick = lax.broadcasted_iota(jnp.int32, (1, n_slots), 1) == slot_ref[...]
     weight = jnp.sum(jnp.where(pick, qw_ref[...], 0.0), axis=1, keepdims=True)
     back = jnp.concatenate([diag_ref[1, steps - 1 - s : steps - s, :] for s in range(steps)], axis=0)
-    redbuf[e] = weight * (diag_ref[0] + back - full_ref[...])
+    near = 2 if n_energy % 2 == 0 else 1
+    far = n_energy // near
+    zed = e // near
+    ring = near * n_layer
+    own = lax.rem(lin, ring)
+    zbuf[zed] = weight * (diag_ref[0] + back - full_ref[...])
 
     def exchange(buf, me, count, place, send_sem, recv_sem):
         def send(k, c):
@@ -254,29 +271,29 @@
             src_ref=rest, dst_ref=rest, send_sem=send_sem, recv_sem=recv_sem,
             device_id=place(lax.rem(me + 1, count)), device_id_type=LOGICAL)
 
-    def ordered_sum(ref, count):
+    def ordered_sum(ref, count, start=0, stride=1):
         if count <= 8:
-            out = ref[0]
+            out = ref[start]
             for k in range(1, count):
-                out = out + ref[k]
+                out = out + ref[start + k * stride]
             return out
-        return lax.fori_loop(1, count, lambda k, c: c + ref[k], ref[0])
-
-    red = exchange(redbuf, e, n_energy, lambda p: p * n_layer + i, red_send, red_recv)
+        return lax.fori_loop(1, count, lambda k, c: c + ref[start + k * stride], ref[start])
+
+    wide = exchange(zbuf, zed, far, lambda p: p * ring + own, z_send, z_recv)
+    wide.wait_recv()
+    redbuf[own] = ordered_sum(zbuf, far)
+    red = exchange(redbuf, own, ring, lambda p: zed * ring + p, red_send, red_recv)
+    wide.wait_send()
     red.wait_recv()
-    own = ordered_sum(redbuf, n_energy)
-    dens_ref[...] = own
-    rows_buf[i] = own
-    row = exchange(rows_buf, i, n_layer, lambda p: e * n_layer + p, row_send, row_recv)
     red.wait_send()
-    row.wait_recv()
-    row.wait_send()
+    rows = [ordered_sum(redbuf, near, k, n_layer) for k in range(n_layer)]
+    dens_ref[...] = ordered_sum(redbuf, near, i, n_layer)
 
     dop_ext[halo : halo + planes] = dop_ref[...]
     scr_ext[halo : halo + planes] = scr_ref[...]
     for copy in halo_copies:
         copy.wait_recv()
-    rows = rows_buf[...].reshape(n_layer * steps, m)
+    rows = jnp.concatenate(rows, axis=0)
     orb_z = m // ORB_Y
     padded = -(-ext // 8) * 8
     first_plane = lin * planes - halo
@@ -325,8 +342,8 @@
 
         @pl.when(pos < n_layer - 1)
         def _():
-            relay_copy(side, 0).wait_send()
-            relay_copy(side, 1).wait_send()
+            for part in range(2):
+                relay_copy(side, part, gout.at[side]).wait_send()
 
     sums.wait_recv()
     gram = jnp.sum(mom[...].reshape(total, nz), axis=0, keepdims=True)
@@ -395,20 +412,23 @@
     call = pl.pallas_call(
         functools.partial(kernel, n_energy, n_layer),
         out_shape=(pltpu.VMEM((steps, m), F32), pltpu.VMEM(doping.shape, F32), pltpu.VMEM(doping.shape, F32)),
-        in_specs=[anym] * 5 + [vmem] + [anym] * 3,
+        in_specs=[anym] * 9,
         out_specs=(vmem, vmem, vmem),
         scratch_shapes=[
             pltpu.VMEM((steps, m, m), F32),
             pltpu.VMEM((m, m), F32),
             pltpu.VMEM((1,) + quad_weight.shape, F32),
+            pltpu.VMEM((1, 1), jnp.int32),
             pltpu.VMEM((1,) + plane_of.shape, jnp.int32),
             pltpu.VMEM(doping.shape, F32),
             pltpu.VMEM(doping.shape, F32),
-            dma((steps + 7,)),
-            pltpu.VMEM((2, 4, m, m), BF16),
+            dma((steps + 8,)),
+            pltpu.VMEM((2, 2, 2, m, m), BF16),
+            pltpu.VMEM((2, m, m), F32),
+            pltpu.VMEM((2, steps, 2, m, m), BF16),
+            pltpu.VMEM((2, 2, m, m), BF16),
             pltpu.VMEM((2, steps, m, m), F32),
-            pltpu.VMEM((2, m, m), F32),
-            pltpu.VMEM((2, m, m), F32),
+            pltpu.VMEM((2, m, m), BF16),
             pltpu.VMEM((2, steps, m), F32),
             pltpu.VMEM((steps, m), F32),
             pltpu.VMEM((2, m, m), F32),
@@ -416,7 +436,7 @@
             pltpu.VMEM((ext, ny, nz), F32),
             pltpu.VMEM((ext, ny, nz), F32),
             pltpu.VMEM((n_energy, steps, m), F32),
-            pltpu.VMEM((n_layer, steps, m), F32),
+            pltpu.VMEM((2 * n_layer, steps, m), F32),
             pltpu.VMEM((n_energy * n_layer, 1, nz), F32),
             dma((2, 2)), dma((2, 2)), dma((4,)), dma((4,)),
             dma, dma, dma, dma, dma, dma,

time: 37.8 us -> 36 us (0.952)
  Pallas kernels: 36.3 us -> 34.6 us
    pallas_call x1, Pallas kernels: 35.5 us -> 33.8 us  [body(): call(layer_inverse[0], coupling, lead_left[0], lead_right[0], quad_weight...]
where the time goes in v2:
time: 36 us; the launch traced here: 35.9 us
  Pallas kernels  34.6 us (96%)
  between operations  1.29 us (4%)
    pallas_call x1, Pallas kernels, body(): call(layer_inverse[0], coupling, lead_left[0], lead_right[0], quad_weight...  33.8 us
    pallas_call x1, Pallas kernels, body(): pl.pallas_call(put, out_shape=tuple((jax.ShapeDtypeStruct(x.shape, F32) f...  0.82 us

profile of v2, /device:TPU:0, one launch (start us, length us, event | category | flops | bytes accessed | tf_op | source)
XLA Modules:
  0.0 35.9 jit_solution(1967585700847798417)
XLA Ops:
  1.3 33.8 %shard_map.112 = (f32[8,256]{1,0:T(8,128)S(1)}, f32[4,128,128]{2,1,0:T(8,128)S(1)}, f32[4,128,128]{2,1,0:T(8,128)S(1)}) custom-call(f32[8,256,256]{2,1,0:T(8,128)} %bitcast.7, f32[256,256]{1,0:T(8,128)} %t_hbm.1, f32[256,256]{1,0:T(8,128)} %bitcast.8, f32[256,256]{1,0:T(8,128)} %bitcast.9, f32[1,8]{1,0:T(1,128)} %bitcast.10, s32[1,1]{1,0:T(1,128)} %bitcast.6.slot_hbm, ...), custom_call_target="tpu_custom_call" | custom-call | tf_op jit(solution)/shard_map/pallas_call | solution.py:448
  35.1 0.8 %shard_map.113 = (f32[8,256]{1,0:T(8,128)}, f32[4,128,128]{2,1,0:T(8,128)}, f32[4,128,128]{2,1,0:T(8,128)}) custom-call(f32[8,256]{1,0:T(8,128)S(1)} %get-tuple-element.6.dens_ref, f32[4,128,128]{2,1,0:T(8,128)S(1)} %get-tuple-element.7.pot_ref, f32[4,128,128]{2,1,0:T(8,128)S(1)} %get-tuple-element.8.res_ref), custom_call_target="tpu_custom_call" | custom-call | tf_op jit(solution)/shard_map/pallas_call | solution.py:452

commit v3 on v2

--- a/solution.py
+++ b/solution.py
@@ -41,17 +41,16 @@
         lax.fori_loop(1, count, step, 0)
 
 
-def beside_of(v, prev_z, next_z):
-    inner = v[1:-1]
-    n, ny, nz = inner.shape
-    total = v[2:] + v[:-2]
-    yi = lax.broadcasted_iota(jnp.int32, (1, ny, 1), 1)
-    zi = lax.broadcasted_iota(jnp.int32, (1, 1, nz), 2)
-    total += jnp.where(yi == 0, 0.0, pltpu.roll(inner, 1, 1))
-    total += jnp.where(yi == ny - 1, 0.0, pltpu.roll(inner, ny - 1, 1))
-    total += jnp.where(zi == 0, 0.0, pltpu.roll(inner, 1, 2))
-    total += jnp.where(zi == nz - 1, 0.0, pltpu.roll(inner, nz - 1, 2))
-    return total
+def around(x):
+    ny, nz = x.shape
+    row = lax.broadcasted_iota(jnp.int32, (8, nz), 0)
+    lane = lax.broadcasted_iota(jnp.int32, (1, nz), 1)
+    up, down = pltpu.roll(x, 1, 0), pltpu.roll(x, ny - 1, 0)
+    up = jnp.concatenate([jnp.where(row == 0, 0.0, up[:8]), up[8:]], axis=0)
+    down = jnp.concatenate([down[:-8], jnp.where(row == 7, 0.0, down[-8:])], axis=0)
+    left, right = pltpu.roll(x, 1, 1), pltpu.roll(x, nz - 1, 1)
+    sides = jnp.where(lane == 0, right, jnp.where(lane == nz - 1, left, left + right))
+    return (up + down) + sides
 
 
 def kernel(
@@ -60,7 +59,7 @@
     dens_ref, pot_ref, res_ref,
     d_ref, t_ref, qw_ref, slot_ref, plane_ref, dop_ref, scr_ref, in_sem,
     p_ref, s_ref, ct_ref, c_ref, w_ref, x_ref, diag_ref, full_ref, gin, gout, dop_ext, scr_ext,
-    zbuf, redbuf, mom,
+    v_ref, coef_ref, spread_ref, zbuf, redbuf, mom,
     relay_send, relay_recv, halo_send, halo_recv,
     z_send, z_recv, red_send, red_recv, mom_send, mom_recv,
 ):
@@ -171,13 +170,18 @@
 
     for s in range(steps):
         props = [pair(p_ref, (side, s % 2)) for side in range(2)]
-        halves = [mm3(props[side], split(s_ref[side])) for side in range(2)]
+        halves = []
+        for side in range(2):
+            s_hi, s_lo = split(s_ref[side])
+            halves.append(mm(props[side][0], s_hi) + mm(props[side][0], s_lo))
         if s < last:
             for side in range(2):
                 prepare(s + 1, side)
         for side in range(2):
             d = d_ref[layer_of(side, s)]
-            acc = d + mm3(split(halves[side]), props[side], mmt)
+            hi, lo = split(halves[side])
+            cross = mmt(hi, props[side][1])
+            acc = d + (mmt(hi, props[side][0]) + mmt(lo, props[side][0])) + (cross + cross.T)
             s_ref[side] = acc
             diag_ref[side, s : s + 1, :] = diag_row(acc)
             if side == 0:
@@ -216,9 +220,27 @@
 
     first = (2 * i) // n_layer
 
+    first_plane = lin * planes - halo
+
+    def inside(q):
+        return jnp.logical_and(first_plane + q >= 0, first_plane + q < total * planes)
+
     def turn_step(turn, c):
         side = first + turn * (1 - 2 * first)
         pos = i + side * (n_layer - 1 - 2 * i)
+
+        @pl.when(turn == 1)
+        def _():
+            for copy in halo_copies:
+                copy.wait_recv()
+            for q in range(ext):
+                keep = inside(q)
+                own = halo <= q < halo + planes
+                dop = dop_ref[q - halo] if own else dop_ext[q]
+                dop_ext[q] = jnp.where(keep, dop, 0.0)
+                if 0 < q < ext - 1:
+                    scr = scr_ref[q - halo] if own else scr_ext[q]
+                    coef_ref[q] = jnp.where(keep, (6.0 - CENTER + scr) * (1.0 / HALF), 0.0)
 
         @pl.when(pos > 0)
         def _():
@@ -289,48 +311,44 @@
     rows = [ordered_sum(redbuf, near, k, n_layer) for k in range(n_layer)]
     dens_ref[...] = ordered_sum(redbuf, near, i, n_layer)
 
-    dop_ext[halo : halo + planes] = dop_ref[...]
-    scr_ext[halo : halo + planes] = scr_ref[...]
-    for copy in halo_copies:
-        copy.wait_recv()
-    rows = jnp.concatenate(rows, axis=0)
+    rows = split(jnp.concatenate(rows, axis=0))
     orb_z = m // ORB_Y
     padded = -(-ext // 8) * 8
-    first_plane = lin * planes - halo
     ids = first_plane + lax.broadcasted_iota(jnp.int32, (padded, 1), 0)
-    onehot = (plane_ref[...] == ids).astype(F32)
-    charge_rows = jnp.dot(onehot, rows, precision=lax.Precision.HIGHEST, preferred_element_type=F32)
-    ysel = (lax.broadcasted_iota(jnp.int32, (ny, m), 1) // orb_z
-            == lax.broadcasted_iota(jnp.int32, (ny, m), 0) // (ny // ORB_Y))
+    onehot = (plane_ref[...] == ids).astype(F32).astype(BF16)
+    charge_rows = mm(onehot, rows[0]) + mm(onehot, rows[1])
+    ysel = (lax.broadcasted_iota(jnp.int32, (ORB_Y, m), 1) // orb_z
+            == lax.broadcasted_iota(jnp.int32, (ORB_Y, m), 0))
     zsel = (lax.broadcasted_iota(jnp.int32, (m, nz), 1) // (nz // orb_z)
             == lax.rem(lax.broadcasted_iota(jnp.int32, (m, nz), 0), orb_z)).astype(BF16)
-    spreads = jnp.concatenate(
-        [jnp.where(ysel, charge_rows[p : p + 1, :], 0.0) for p in range(ext)], axis=0)
-    hi, lo = split(spreads)
-    charge = (mm(hi, zsel) + mm(lo, zsel)).reshape(ext, ny, nz)
-    last_plane = total * planes
-    gid = first_plane + lax.broadcasted_iota(jnp.int32, (ext, 1, 1), 0)
-    inside = jnp.logical_and(gid >= 0, gid < last_plane)
-    v0 = jnp.where(inside, charge - dop_ext[...], 0.0)
-
-    basis = [v0]
-    for k in range(CG_ITERS):
-        prev = basis[-1]
-        scr = scr_ext[k + 1 : ext - k - 1]
-        shifted = ((6.0 - CENTER + scr) * prev[1:-1] - beside_of(prev, None, None)) * (1.0 / HALF)
-        if k > 0:
-            shifted = 2.0 * shifted - basis[-2][2:-2]
-        mask = inside[k + 1 : ext - k - 1]
-        basis.append(jnp.where(mask, shifted, 0.0))
-    own_v = [b[halo - k : halo - k + planes] for k, b in enumerate(basis)]
-    names, parts = {}, []
-    for a in range(CG_ITERS):
-        for b in range(a, CG_ITERS + 1):
-            names[a, b] = len(parts)
-            parts.append(jnp.sum(own_v[a] * own_v[b], axis=(0, 1), keepdims=True)[0])
-    parts.append(jnp.zeros((16 - len(parts), nz), F32))
+    spreads = split(jnp.concatenate(
+        [jnp.where(ysel, charge_rows[p : p + 1, :], 0.0) for p in range(ext)], axis=0))
+    spread_ref[...] = mm(spreads[0], zsel) + mm(spreads[1], zsel)
+    patch = ny // ORB_Y
+    for q in range(ext):
+        charge = [jnp.broadcast_to(spread_ref[q * ORB_Y + y : q * ORB_Y + y + 1, :], (patch, nz)) for y in range(ORB_Y)]
+        v_ref[0, q] = jnp.concatenate(charge, axis=0) - dop_ext[q]
+    for k in range(1, CG_ITERS + 1):
+        twice = 1.0 if k == 1 else 2.0
+        for q in range(k, ext - k):
+            scale = jnp.where(inside(q), twice / HALF, 0.0)
+            x = v_ref[k - 1, q]
+            near_sum = (v_ref[k - 1, q - 1] + v_ref[k - 1, q + 1]) + around(x)
+            out = twice * coef_ref[q] * x - scale * near_sum
+            v_ref[k, q] = out if k == 1 else out - v_ref[k - 2, q]
+
+    def dot_of(a, b):
+        out = 0.0
+        for q in range(halo, halo + planes):
+            prod = v_ref[a, q] * v_ref[b, q]
+            out = out + jnp.sum(prod.reshape(ny // 8, 8, nz), axis=0)
+        return jnp.sum(out, axis=0, keepdims=True)
+
+    pairs = [(0, k) for k in range(CG_ITERS + 1)] + [(CG_ITERS - 1, k) for k in range(CG_ITERS - 1, CG_ITERS + 1)]
+    parts = [dot_of(a, b) for a, b in pairs]
+    parts.append(jnp.zeros((8 - len(parts), nz), F32))
     column = jnp.sum(jnp.concatenate(parts, axis=0), axis=1, keepdims=True)
-    spot = lax.broadcasted_iota(jnp.int32, (16, nz), 0) == lax.broadcasted_iota(jnp.int32, (16, nz), 1)
+    spot = lax.broadcasted_iota(jnp.int32, (8, nz), 0) == lax.broadcasted_iota(jnp.int32, (8, nz), 1)
     mom[lin] = jnp.sum(jnp.where(spot, column, 0.0), axis=0, keepdims=True)
 
     sums = exchange(mom, lin, total, lambda p: p, mom_send, mom_recv)
@@ -348,9 +366,12 @@
     sums.wait_recv()
     gram = jnp.sum(mom[...].reshape(total, nz), axis=0, keepdims=True)
 
+    base = [gram[:, k : k + 1] for k in range(len(pairs))]
+    moments = base[: CG_ITERS + 1]
+    moments += [2.0 * base[CG_ITERS + 1 + k] - moments[k] for k in range(2)]
+
     def entry(a, b):
-        k = names[min(a, b), max(a, b)]
-        return gram[:, k : k + 1]
+        return 0.5 * (moments[a + b] + moments[abs(a - b)])
 
     def inner(x, y):
         terms = [x[a] * y[b] * entry(a, b) for a in x for b in y]
@@ -386,8 +407,9 @@
             norm = new
 
     for coefs, out in ((pot, pot_ref), (res, res_ref)):
-        terms = [coefs[k][None] * own_v[k] for k in coefs]
-        out[...] = functools.reduce(lambda p, q: p + q, terms)
+        for q in range(planes):
+            terms = [coefs[k] * v_ref[k, halo + q] for k in coefs]
+            out[q] = functools.reduce(lambda p, q: p + q, terms)
 
 
 def put(dens_ref, pot_ref, res_ref, dens_hbm, pot_hbm, res_hbm, sem):
@@ -435,6 +457,9 @@
             pltpu.VMEM((2, m, m), F32),
             pltpu.VMEM((ext, ny, nz), F32),
             pltpu.VMEM((ext, ny, nz), F32),
+            pltpu.VMEM((CG_ITERS + 1, ext, ny, nz), F32),
+            pltpu.VMEM((ext, ny, nz), F32),
+            pltpu.VMEM((ext * ORB_Y, nz), F32),
             pltpu.VMEM((n_energy, steps, m), F32),
             pltpu.VMEM((2 * n_layer, steps, m), F32),
             pltpu.VMEM((n_energy * n_layer, 1, nz), F32),

time: 36 us -> 35.5 us (0.986)
  Pallas kernels: 34.6 us -> 34 us
    pallas_call x1, Pallas kernels: 33.8 us -> 33.2 us  [body(): call(layer_inverse[0], coupling, lead_left[0], lead_right[0], quad_weight...]
where the time goes in v3:
time: 35.5 us; the launch traced here: 35.3 us
  Pallas kernels  34 us (96%)
  between operations  1.29 us (4%)
    pallas_call x1, Pallas kernels, body(): call(layer_inverse[0], coupling, lead_left[0], lead_right[0], quad_weight...  33.2 us
    pallas_call x1, Pallas kernels, body(): pl.pallas_call(put, out_shape=tuple((jax.ShapeDtypeStruct(x.shape, F32) f...  0.82 us

profile of v3, /device:TPU:0, one launch (start us, length us, event | category | flops | bytes accessed | tf_op | source)
XLA Modules:
  0.0 35.3 jit_solution(1932501409836174579)
XLA Ops:
  1.3 33.2 %shard_map.112 = (f32[8,256]{1,0:T(8,128)S(1)}, f32[4,128,128]{2,1,0:T(8,128)S(1)}, f32[4,128,128]{2,1,0:T(8,128)S(1)}) custom-call(f32[8,256,256]{2,1,0:T(8,128)} %bitcast.7, f32[256,256]{1,0:T(8,128)} %t_hbm.1, f32[256,256]{1,0:T(8,128)} %bitcast.8, f32[256,256]{1,0:T(8,128)} %bitcast.9, f32[1,8]{1,0:T(1,128)} %bitcast.10, s32[1,1]{1,0:T(1,128)} %bitcast.6.slot_hbm, ...), custom_call_target="tpu_custom_call" | custom-call | tf_op jit(solution)/shard_map/pallas_call | solution.py:473
  34.5 0.8 %shard_map.113 = (f32[8,256]{1,0:T(8,128)}, f32[4,128,128]{2,1,0:T(8,128)}, f32[4,128,128]{2,1,0:T(8,128)}) custom-call(f32[8,256]{1,0:T(8,128)S(1)} %get-tuple-element.6.dens_ref, f32[4,128,128]{2,1,0:T(8,128)S(1)} %get-tuple-element.7.pot_ref, f32[4,128,128]{2,1,0:T(8,128)S(1)} %get-tuple-element.8.res_ref), custom_call_target="tpu_custom_call" | custom-call | tf_op jit(solution)/shard_map/pallas_call | solution.py:477

commit v4 on v3

--- a/solution.py
+++ b/solution.py
@@ -59,8 +59,8 @@
     dens_ref, pot_ref, res_ref,
     d_ref, t_ref, qw_ref, slot_ref, plane_ref, dop_ref, scr_ref, in_sem,
     p_ref, s_ref, ct_ref, c_ref, w_ref, x_ref, diag_ref, full_ref, gin, gout, dop_ext, scr_ext,
-    v_ref, coef_ref, spread_ref, zbuf, redbuf, mom,
-    relay_send, relay_recv, halo_send, halo_recv,
+    v_ref, coef_ref, spread_ref, zbuf, redbuf, mom, pair_ref,
+    pair_send, pair_recv, relay_send, relay_recv, halo_send, halo_recv,
     z_send, z_recv, red_send, red_recv, mom_send, mom_recv,
 ):
     steps, m, _ = d_hbm.shape
@@ -168,6 +168,7 @@
     for side in range(2):
         pl.when(i == ends[side])(lead_copy(side).wait)
 
+    pairs = n_layer == 4
     for s in range(steps):
         props = [pair(p_ref, (side, s % 2)) for side in range(2)]
         halves = []
@@ -193,7 +194,10 @@
                 ct_ref[side, 0, 1] = lo
                 w_ref[side, 0] = hi.astype(F32) + 2.0 * lo.astype(F32)
             else:
-                store_carry(s, side, mm3(pair(ct_ref, (side, s - 1)), props[side], mmt))
+                ct = mm3(pair(ct_ref, (side, s - 1)), props[side], mmt)
+                store_carry(s, side, ct)
+                if pairs and s == last:
+                    gout[side] = ct
         if s == 1:
             pl.semaphore_wait(barrier, total - 1)
             for copy in grid_copies:
@@ -213,6 +217,19 @@
         def _():
             for part in range(2):
                 relay_copy(side, part, s_ref.at[side]).start()
+
+    def pair_copy(side, part):
+        return pltpu.make_async_remote_copy(
+            src_ref=(s_ref, gout)[part].at[side], dst_ref=pair_ref.at[part],
+            send_sem=pair_send.at[part], recv_sem=pair_recv.at[part],
+            device_id=e * n_layer + lax.rem(i + 1 - 2 * side + n_layer, n_layer), device_id_type=LOGICAL)
+
+    if pairs:
+        for side in range(2):
+            @pl.when(i == 2 - side)
+            def _():
+                for part in range(2):
+                    pair_copy(side, part).start()
 
     for side in range(2):
         for part in range(2):
@@ -242,28 +259,66 @@
                     scr = scr_ref[q - halo] if own else scr_ext[q]
                     coef_ref[q] = jnp.where(keep, (6.0 - CENTER + scr) * (1.0 / HALF), 0.0)
 
-        @pl.when(pos > 0)
-        def _():
-            relay_copy(side, 0, gout.at[side]).wait_recv()
-            gin[side, h:, :h] = gin[side, :h, h:].T
-            relay_copy(side, 1, gout.at[side]).wait_recv()
-            for part, x in enumerate(split(gin[side])):
-                x_ref[part] = x
-
-            @pl.when(pos < n_layer - 1)
+        if pairs:
+            @pl.when(pos == 3)
             def _():
-                half = split(mm3((x_ref[0], x_ref[1]), pair(ct_ref, (side, last))))
-                outer = pair(c_ref, (side,))
-                gout[side, :h, :] = s_ref[side, :h, :] + mm3([x[:h] for x in outer], half)
-                relay_copy(side, 0, gout.at[side]).start()
-                gout[side, h:, h:] = (
-                    s_ref[side, h:, h:] + mm3([x[h:] for x in outer], [x[:, h:] for x in half]))
-                relay_copy(side, 1, gout.at[side]).start()
-
+                for part in range(2):
+                    pair_copy(side, part).wait_recv()
+                below = split(pair_ref[0])
+                outer = split(pair_ref[1])
+                for s in range(steps):
+                    cur = pair(ct_ref, (side, s))
+                    z = mm(below[0], cur[0]) + mm(below[1], cur[0])
+                    diag_ref[side, s : s + 1, :] += jnp.sum(z * w_ref[side, s], axis=0, keepdims=True)
+                    store_carry(s, side, mm3(outer, cur))
+
+        relays = pos == 1 if pairs else jnp.logical_and(pos > 0, pos < n_layer - 1)
+        ends_here = pos > 1 if pairs else pos == n_layer - 1
+
+        def take(part):
+            relay_copy(side, part, gout.at[side]).wait_recv()
+
+        def fill(part):
+            rows = slice(0, h) if part == 0 else slice(h, m)
+            if part == 1:
+                gin[side, h:, :h] = gin[side, :h, h:].T
+            for k, x in enumerate(split(gin[side, rows, :])):
+                x_ref[k, rows, :] = x
+
+        def forward(part):
+            if pairs:
+                @pl.when(pos == 2)
+                def _():
+                    relay_copy(side, part, gin.at[side]).start()
+
+        def apply(part):
+            rows = slice(0, h) if part == 0 else slice(h, m)
             for s in range(steps):
                 carry = ct_ref[side, s, 0]
-                z = mm(x_ref[0], carry) + mm(x_ref[1], carry)
-                diag_ref[side, s : s + 1, :] += jnp.sum(z * w_ref[side, s], axis=0, keepdims=True)
+                z = mm(x_ref[0, rows, :], carry) + mm(x_ref[1, rows, :], carry)
+                diag_ref[side, s : s + 1, :] += jnp.sum(z * w_ref[side, s, rows, :], axis=0, keepdims=True)
+
+        @pl.when(relays)
+        def _():
+            for part in range(2):
+                take(part)
+                fill(part)
+            half = split(mm3((x_ref[0], x_ref[1]), pair(ct_ref, (side, last))))
+            outer = pair(c_ref, (side,))
+            gout[side, :h, :] = s_ref[side, :h, :] + mm3([x[:h] for x in outer], half)
+            relay_copy(side, 0, gout.at[side]).start()
+            gout[side, h:, h:] = (
+                s_ref[side, h:, h:] + mm3([x[h:] for x in outer], [x[:, h:] for x in half]))
+            relay_copy(side, 1, gout.at[side]).start()
+
+        for part in range(2):
+            @pl.when(ends_here)
+            def _():
+                take(part)
+                forward(part)
+                fill(part)
+
+            pl.when(pos > 0)(functools.partial(apply, part))
 
         return c
 
@@ -362,6 +417,13 @@
         def _():
             for part in range(2):
                 relay_copy(side, part, gout.at[side]).wait_send()
+
+    if pairs:
+        for side in range(2):
+            @pl.when(i == 2 - side)
+            def _():
+                for part in range(2):
+                    pair_copy(side, part).wait_send()
 
     sums.wait_recv()
     gram = jnp.sum(mom[...].reshape(total, nz), axis=0, keepdims=True)
@@ -463,6 +525,8 @@
             pltpu.VMEM((n_energy, steps, m), F32),
             pltpu.VMEM((2 * n_layer, steps, m), F32),
             pltpu.VMEM((n_energy * n_layer, 1, nz), F32),
+            pltpu.VMEM((2, m, m), F32),
+            dma((2,)), dma((2,)),
             dma((2, 2)), dma((2, 2)), dma((4,)), dma((4,)),
             dma, dma, dma, dma, dma, dma,
         ],

time: 35.5 us -> 34.5 us (0.972)
  Pallas kernels: 34 us -> 33.1 us
    pallas_call x1, Pallas kernels: 33.2 us -> 32.2 us  [body(): call(layer_inverse[0], coupling, lead_left[0], lead_right[0], quad_weight...]
where the time goes in v4:
time: 34.5 us; the launch traced here: 34.3 us
  Pallas kernels  33.1 us (96%)
  between operations  1.29 us (4%)
    pallas_call x1, Pallas kernels, body(): call(layer_inverse[0], coupling, lead_left[0], lead_right[0], quad_weight...  32.2 us
    pallas_call x1, Pallas kernels, body(): pl.pallas_call(put, out_shape=tuple((jax.ShapeDtypeStruct(x.shape, F32) f...  0.82 us

profile of v4, /device:TPU:0, one launch (start us, length us, event | category | flops | bytes accessed | tf_op | source)
XLA Modules:
  0.0 34.3 jit_solution(15935512153085312551)
XLA Ops:
  1.3 32.2 %shard_map.112 = (f32[8,256]{1,0:T(8,128)S(1)}, f32[4,128,128]{2,1,0:T(8,128)S(1)}, f32[4,128,128]{2,1,0:T(8,128)S(1)}) custom-call(f32[8,256,256]{2,1,0:T(8,128)} %bitcast.7, f32[256,256]{1,0:T(8,128)} %t_hbm.1, f32[256,256]{1,0:T(8,128)} %bitcast.8, f32[256,256]{1,0:T(8,128)} %bitcast.9, f32[1,8]{1,0:T(1,128)} %bitcast.10, s32[1,1]{1,0:T(1,128)} %bitcast.6.slot_hbm, ...), custom_call_target="tpu_custom_call" | custom-call | tf_op jit(solution)/shard_map/pallas_call | solution.py:537
  33.5 0.8 %shard_map.113 = (f32[8,256]{1,0:T(8,128)}, f32[4,128,128]{2,1,0:T(8,128)}, f32[4,128,128]{2,1,0:T(8,128)}) custom-call(f32[8,256]{1,0:T(8,128)S(1)} %get-tuple-element.6.dens_ref, f32[4,128,128]{2,1,0:T(8,128)S(1)} %get-tuple-element.7.pot_ref, f32[4,128,128]{2,1,0:T(8,128)S(1)} %get-tuple-element.8.res_ref), custom_call_target="tpu_custom_call" | custom-call | tf_op jit(solution)/shard_map/pallas_call | solution.py:541

commit v5 on v4

--- a/solution.py
+++ b/solution.py
@@ -87,6 +87,7 @@
         return pltpu.make_async_copy((lead_l_hbm, lead_r_hbm)[side], s_ref.at[side], in_sem.at[steps + 2 + side])
 
     ends = (0, n_layer - 1)
+    at_end = jnp.logical_or(i == 0, i == n_layer - 1)
     for s in order[:2]:
         layer_copy(s).start()
     for side in range(2):
@@ -123,9 +124,7 @@
             device_id=down, device_id_type=LOGICAL))
 
     t_copy.wait()
-    t = t_ref[...]
-    tt = t.T
-    t, tt = split(t), split(tt)
+    t = split(t_ref[...])
     eye = (lax.broadcasted_iota(jnp.int32, (m // 2, m // 2), 0)
            == lax.broadcasted_iota(jnp.int32, (m // 2, m // 2), 1))
 
@@ -134,7 +133,7 @@
         tiles = [jnp.where(eye, x[k * h : k * h + h, k * h : k * h + h], 0.0) for k in range(2)]
         return jnp.concatenate([jnp.sum(tile, axis=0, keepdims=True) for tile in tiles], axis=1)
 
-    sides = ((t, tt), (tt, t))
+    dots = (mm, mmt)
     h = m // 2
     last = steps - 1
 
@@ -145,7 +144,7 @@
         return ref[at + (0,)], ref[at + (1,)]
 
     def prepare(s, side):
-        prop = mm3(split(d_ref[layer_of(side, s)]), sides[side][0])
+        prop = mm3(split(d_ref[layer_of(side, s)]), t, dots[side])
         for j, x in enumerate(split(prop)):
             p_ref[side, s % 2, j] = x
 
@@ -167,6 +166,13 @@
         layer_copy(s).wait()
     for side in range(2):
         pl.when(i == ends[side])(lead_copy(side).wait)
+
+    def relay_copy(side, part, buf):
+        spot = (pl.ds(0, h), pl.ds(0, m)) if part == 0 else (pl.ds(h, h), pl.ds(h, h))
+        return pltpu.make_async_remote_copy(
+            src_ref=buf.at[spot], dst_ref=gin.at[(side,) + spot],
+            send_sem=relay_send.at[side, part], recv_sem=relay_recv.at[side, part],
+            device_id=e * n_layer + lax.rem(i + 1 - 2 * side + n_layer, n_layer), device_id_type=LOGICAL)
 
     pairs = n_layer == 4
     for s in range(steps):
@@ -187,6 +193,12 @@
             diag_ref[side, s : s + 1, :] = diag_row(acc)
             if side == 0:
                 full_ref[s : s + 1, :] = diag_row(d)
+        if s == last:
+            for side in range(2):
+                @pl.when(i == ends[side])
+                def _():
+                    for part in range(2):
+                        relay_copy(side, part, s_ref.at[side]).start()
         for side in range(2):
             if s == 0:
                 hi, lo = (x.T for x in props[side])
@@ -194,29 +206,18 @@
                 ct_ref[side, 0, 1] = lo
                 w_ref[side, 0] = hi.astype(F32) + 2.0 * lo.astype(F32)
             else:
-                ct = mm3(pair(ct_ref, (side, s - 1)), props[side], mmt)
-                store_carry(s, side, ct)
-                if pairs and s == last:
-                    gout[side] = ct
+                store_carry(s, side, mm3(pair(ct_ref, (side, s - 1)), props[side], mmt))
         if s == 1:
             pl.semaphore_wait(barrier, total - 1)
             for copy in grid_copies:
                 copy.wait()
-            for copy in halo_copies:
+            for copy in halo_copies[:2]:
                 copy.start()
 
-    def relay_copy(side, part, buf):
-        spot = (pl.ds(0, h), pl.ds(0, m)) if part == 0 else (pl.ds(h, h), pl.ds(h, h))
-        return pltpu.make_async_remote_copy(
-            src_ref=buf.at[spot], dst_ref=gin.at[(side,) + spot],
-            send_sem=relay_send.at[side, part], recv_sem=relay_recv.at[side, part],
-            device_id=e * n_layer + lax.rem(i + 1 - 2 * side + n_layer, n_layer), device_id_type=LOGICAL)
-
-    for side in range(2):
-        @pl.when(i == ends[side])
-        def _():
-            for part in range(2):
-                relay_copy(side, part, s_ref.at[side]).start()
+            @pl.when(at_end)
+            def _():
+                for copy in halo_copies[2:]:
+                    copy.start()
 
     def pair_copy(side, part):
         return pltpu.make_async_remote_copy(
@@ -228,6 +229,8 @@
         for side in range(2):
             @pl.when(i == 2 - side)
             def _():
+                hi, lo = pair(ct_ref, (side, last))
+                gout[side] = hi.astype(F32) + lo.astype(F32)
                 for part in range(2):
                     pair_copy(side, part).start()
 
@@ -246,18 +249,10 @@
         side = first + turn * (1 - 2 * first)
         pos = i + side * (n_layer - 1 - 2 * i)
 
-        @pl.when(turn == 1)
+        @pl.when(jnp.logical_and(turn == 1, jnp.logical_not(at_end)))
         def _():
-            for copy in halo_copies:
-                copy.wait_recv()
-            for q in range(ext):
-                keep = inside(q)
-                own = halo <= q < halo + planes
-                dop = dop_ref[q - halo] if own else dop_ext[q]
-                dop_ext[q] = jnp.where(keep, dop, 0.0)
-                if 0 < q < ext - 1:
-                    scr = scr_ref[q - halo] if own else scr_ext[q]
-                    coef_ref[q] = jnp.where(keep, (6.0 - CENTER + scr) * (1.0 / HALF), 0.0)
+            for copy in halo_copies[2:]:
+                copy.start()
 
         if pairs:
             @pl.when(pos == 3)
@@ -357,6 +352,16 @@
         return lax.fori_loop(1, count, lambda k, c: c + ref[start + k * stride], ref[start])
 
     wide = exchange(zbuf, zed, far, lambda p: p * ring + own, z_send, z_recv)
+    for copy in halo_copies:
+        copy.wait_recv()
+    for q in range(ext):
+        keep = inside(q)
+        mine = halo <= q < halo + planes
+        dop = dop_ref[q - halo] if mine else dop_ext[q]
+        dop_ext[q] = jnp.where(keep, dop, 0.0)
+        if 0 < q < ext - 1:
+            scr = scr_ref[q - halo] if mine else scr_ext[q]
+            coef_ref[q] = jnp.where(keep, (6.0 - CENTER + scr) * (1.0 / HALF), 0.0)
     wide.wait_recv()
     redbuf[own] = ordered_sum(zbuf, far)
     red = exchange(redbuf, own, ring, lambda p: zed * ring + p, red_send, red_recv)

time: 34.5 us -> 34.3 us (level)
  no operation moved by 1% of the time
where the time goes in v5:
time: 34.3 us; the launch traced here: 34.1 us
  Pallas kernels  32.8 us (96%)
  between operations  1.29 us (4%)
    pallas_call x1, Pallas kernels, body(): call(layer_inverse[0], coupling, lead_left[0], lead_right[0], quad_weight...  32 us
    pallas_call x1, Pallas kernels, body(): pl.pallas_call(put, out_shape=tuple((jax.ShapeDtypeStruct(x.shape, F32) f...  0.82 us

profile of v5, /device:TPU:0, one launch (start us, length us, event | category | flops | bytes accessed | tf_op | source)
XLA Modules:
  0.0 34.1 jit_solution(15150939213045153374)
XLA Ops:
  1.3 32.0 %shard_map.112 = (f32[8,256]{1,0:T(8,128)S(1)}, f32[4,128,128]{2,1,0:T(8,128)S(1)}, f32[4,128,128]{2,1,0:T(8,128)S(1)}) custom-call(f32[8,256,256]{2,1,0:T(8,128)} %bitcast.7, f32[256,256]{1,0:T(8,128)} %t_hbm.1, f32[256,256]{1,0:T(8,128)} %bitcast.8, f32[256,256]{1,0:T(8,128)} %bitcast.9, f32[1,8]{1,0:T(1,128)} %bitcast.10, s32[1,1]{1,0:T(1,128)} %bitcast.6.slot_hbm, ...), custom_call_target="tpu_custom_call" | custom-call | tf_op jit(solution)/shard_map/pallas_call | solution.py:542
  33.3 0.8 %shard_map.113 = (f32[8,256]{1,0:T(8,128)}, f32[4,128,128]{2,1,0:T(8,128)}, f32[4,128,128]{2,1,0:T(8,128)}) custom-call(f32[8,256]{1,0:T(8,128)S(1)} %get-tuple-element.6.dens_ref, f32[4,128,128]{2,1,0:T(8,128)S(1)} %get-tuple-element.7.pot_ref, f32[4,128,128]{2,1,0:T(8,128)S(1)} %get-tuple-element.8.res_ref), custom_call_target="tpu_custom_call" | custom-call | tf_op jit(solution)/shard_map/pallas_call | solution.py:546
